TPU v7x, 128 devices: a whole 4x4x4 slice. The times are simulated.
128 devices in a mesh: pipe: 4 (over y_hi, core), exp: 16 (over x, z), pair: 2 (over y_lo).
Axes of the slice: x: 4, y: 4 (y_hi: 2, y_lo: 2; y = y_hi * 2 + y_lo), z: 4, core: 2. Of those that a mesh axis runs over, the one named last changes fastest.
Arguments:
- hidden_in: bfloat16 [4, 1024, 2048], P(None, ('exp', 'pair')), may hold values from -6 to 6
- routes: int32 [4, 4, 1024, 8], P('pipe', None, ('exp', 'pair')), may hold values from 0 to 63, all different within a row; in each aligned block of 32 rows (0 to 31, 32 to 63, ..., all dimensions but the last counted through in order) at most 6 rows name the same one
- gate_probs: float32 [4, 4, 1024, 8], P('pipe', None, ('exp', 'pair')), may hold values from 0.02 to 1
- norm_gain: float32 [4, 2048], P('pipe'), may hold values from 0.1 to 1.9
- w_gate: bfloat16 [4, 64, 2048, 768], P('pipe', ('exp', 'pair')), may hold values from -0.125 to 0.125
- w_up: bfloat16 [4, 64, 2048, 768], P('pipe', ('exp', 'pair')), may hold values from -0.125 to 0.125
- w_down: bfloat16 [4, 64, 768, 2048], P('pipe', ('exp', 'pair')), may hold values from -0.21875 to 0.21875
Outputs:
- layer_outputs: bfloat16 [4, 4, 1024, 2048], P('pipe', None, ('exp', 'pair'))
Inputs may be any that keep to these rules, and one draw needn't show every extreme that they name: `routes`: within each layer and micro-batch, the 32 tokens of one device (aligned blocks) name no expert more than 6 times in all, and each token names 8 different experts.
All inputs are finite; a program needn't handle non-finite values.
Results may differ from a plain program's by a relative error of at most 0.01.
Values may be sent and summed in bfloat16 or wider, within the bound.
A program may use at most 64 MiB of HBM per device.

v0:
```python
import jax
import jax.numpy as jnp
from jax import lax
from jax.sharding import PartitionSpec as P

EPS = 1e-06


def passed_along(value, axis, steps):
    count = lax.axis_size(axis)
    first, last = (max(0, -steps), min(count, count - steps))
    return lax.ppermute(value, axis, [(source, source + steps) for source in range(first, last)])


def expert_block(arrived, wgate, wupper, wdown):
    gate = jnp.einsum("nlcd,ldf->nlcf", arrived, wgate, preferred_element_type=jnp.float32)
    upward = jnp.einsum("nlcd,ldf->nlcf", arrived, wupper, preferred_element_type=jnp.float32)
    hidden = (jax.nn.silu(gate) * upward).astype(jnp.bfloat16)
    return jnp.einsum("nlcf,lfd->nlcd", hidden, wdown, preferred_element_type=jnp.float32).astype(
        jnp.bfloat16
    )


def on_device(hidden_in, routes, gate_probs, norm_gain, w_gate, w_up, w_down):
    section = lax.axis_index("pipe")
    micro, tok_rows, width = hidden_in.shape
    top_count = routes.shape[3]
    groups = lax.axis_size(("exp", "pair"))
    local_experts = w_gate.shape[1]
    experts = local_experts * groups
    capacity = max(2, 3 * tok_rows * top_count // (2 * experts))
    gain = norm_gain[0]
    wgate = w_gate[0]
    wupper = w_up[0]
    wdown = w_down[0]
    expert_ids = jnp.arange(experts, dtype=jnp.int32)

    def layer(state, index):
        chosen = lax.dynamic_index_in_dim(routes[0], index, 0, keepdims=False).reshape(-1)
        probs = lax.dynamic_index_in_dim(gate_probs[0], index, 0, keepdims=False)
        floated = state.astype(jnp.float32)
        scale = lax.rsqrt(jnp.mean(floated * floated, axis=-1, keepdims=True) + EPS)
        normed = (floated * scale * gain).astype(jnp.bfloat16)
        onehot = (chosen[:, None] == expert_ids[None, :]).astype(jnp.int32)
        before = jnp.cumsum(onehot, axis=0) - onehot
        slots = jnp.sum(before * onehot, axis=1)
        outgoing = jnp.zeros((experts, capacity, width), jnp.bfloat16)
        outgoing = outgoing.at[chosen, slots].set(jnp.repeat(normed, top_count, axis=0))
        grouped = outgoing.reshape(groups, local_experts, capacity, width)
        produced = expert_block(
            lax.all_to_all(grouped, ("exp", "pair"), split_axis=0, concat_axis=0, tiled=True),
            wgate,
            wupper,
            wdown,
        )
        returned = lax.all_to_all(
            produced, ("exp", "pair"), split_axis=0, concat_axis=0, tiled=True
        )
        results = returned.reshape(experts, capacity, width)[chosen, slots]
        results = results.reshape(tok_rows, top_count, width).astype(jnp.float32)
        weights = probs / jnp.sum(probs, axis=-1, keepdims=True)
        mixed = jnp.einsum("tk,tkd->td", weights, results)
        return (floated + mixed).astype(jnp.bfloat16)

    def advance(step, carry):
        received, saved = carry
        index = step - section
        valid = jnp.logical_and(index >= 0, index < micro)
        clipped = jnp.clip(index, 0, micro - 1)
        first = lax.dynamic_index_in_dim(hidden_in, clipped, 0, keepdims=False)
        state = jnp.where(section == 0, first, received)
        updated = layer(state, clipped)
        saved = jnp.where(valid, lax.dynamic_update_index_in_dim(saved, updated, clipped, 0), saved)
        received = passed_along(updated, "pipe", 1)
        return (received, saved)

    start = (
        jnp.zeros((tok_rows, width), jnp.bfloat16),
        jnp.zeros((micro, tok_rows, width), jnp.bfloat16),
    )
    received, saved = lax.fori_loop(0, micro + lax.axis_size("pipe") - 1, advance, start)
    return saved[None]


def solution(mesh):
    in_specs = (
        P(None, ("exp", "pair"), None),
        P("pipe", None, ("exp", "pair"), None),
        P("pipe", None, ("exp", "pair"), None),
        P("pipe", None),
        P("pipe", ("exp", "pair"), None, None),
        P("pipe", ("exp", "pair"), None, None),
        P("pipe", ("exp", "pair"), None, None),
    )
    out_specs = P("pipe", None, ("exp", "pair"), None)
    return jax.shard_map(
        on_device, mesh=mesh, in_specs=in_specs, out_specs=out_specs, check_vma=False
    )
```

profile of v0, /device:TPU:1, one launch (start us, length us, event | category | flops | bytes accessed | tf_op | source)
XLA Modules:
  0.0 810.8 jit_solution(4806493436090635416)
XLA Ops:
  0.9 809.9 %while.18 = (s32[]{:T(128)}, bf16[32,2048]{1,0:T(8,128)(2,1)S(1)}, bf16[4,32,2048]{2,1,0:T(8,128)(2,1)}, pred[]{:T(512)}, s32[]{:T(128)}, /*index=5*/bf16[4,32,2...) while((s32[]{:T(128)}, bf16[32,2048]{1,0:T(8,128)(2,1)S(1)}, ...), condition=%wide.region_7.8_spmd.clone.clone, body=%wide.region_0.7_spmd.clone.clone.sunk | while | flops 3630486016 | bytes 61134680 | solution.py:81
  5.1 22.3 %scatter_fusion = bf16[64,6,2048]{2,0,1:T(8,128)(2,1)S(1)} fusion(bf16[64,6,2048]{2,0,1:T(8,128)(2,1)S(1)} %broadcast.267, s32[256]{0:T(256)S(1)} %bitcast.139, bf16[256,2048]{1,0:T(8,128)(2,1)S(1)} %broadcast_bitcast_fusion.2), kind=kCustom, calls=%fused_computation.1.clone.clone.1 | custom fusion | bytes 3147776 | tf_op jit(solution)/shard_map/while/body/eval_jaxpr/scatter | solution.py:48
  30.2 31.6 %all_to_all.26 = bf16[32,2,6,2048]{3,1,2,0:T(2,128)(2,1)S(1)} all-to-all(bf16[32,2,6,2048]{3,1,2,0:T(2,128)(2,1)S(1)} %copy.58), channel_id=1, replica_groups=mesh['pipe'=4,'exp'=16,'pair'=2] {'exp','pair'}, dimensions={0} | all-to-all | bytes 3145728 | tf_op jit(solution)/shard_map/while/body/eval_jaxpr/all_to_all | solution.py:51
  61.8 6.4 fusion.86
  68.2 8.9 %fusion.87 = bf16[32,2,6,2048]{3,0,2,1:T(8,128)(2,1)S(1)} fusion(bf16[2,768,2048]{2,1,0:T(8,128)(2,1)} %get-tuple-element.525, bf16[2,2048,768]{2,1,0:T(8,128)(2,1)} %get-tuple-element.524, bf16[32,2,6,2048]{3,1,2,0:T(2,128)(2,1)S(1)} %all_to_all.26, f32[32,2,6,768]{3,0,2,1:T(8,128)} %fusion.86), kind=kOutput, calls=%fused_computation.10.clone.1 | convolution fusion | flops 2418475008 | bytes 16908288 | tf_op jit(solution)/shard_map/while/body/eval_jaxpr/nlcf,lfd->nlcd/dot_general | solution.py:19
  79.9 4.5 all-to-all-start.1
  84.6 20.7 %all-to-all-done.1 = bf16[32,2,6,2048]{3,1,2,0:T(2,128)(2,1)S(1)} async-done(((bf16[32,2,6,2048]{3,1,2,0:T(2,128)(2,1)}), bf16[32,2,6,2048]{3,1,2,0:T(2,128)(2,1)S(1)}, u32[]{:S(2)}, u32[]{:S(2)}) %all-to-all-start.1) | async-done | bytes 1572896 | tf_op jit(solution)/shard_map/while/body/eval_jaxpr/all_to_all | solution.py:56
  107.1 4.3 gather_fusion
  113.5 7.4 collective-permute-start
  127.1 22.3 %scatter_fusion = bf16[64,6,2048]{2,0,1:T(8,128)(2,1)S(1)} fusion(bf16[64,6,2048]{2,0,1:T(8,128)(2,1)S(1)} %broadcast.267, s32[256]{0:T(256)S(1)} %bitcast.139, bf16[256,2048]{1,0:T(8,128)(2,1)S(1)} %broadcast_bitcast_fusion.2), kind=kCustom, calls=%fused_computation.1.clone.clone.1 | custom fusion | bytes 3147776 | tf_op jit(solution)/shard_map/while/body/eval_jaxpr/scatter | solution.py:48
  152.2 24.8 %all_to_all.26 = bf16[32,2,6,2048]{3,1,2,0:T(2,128)(2,1)S(1)} all-to-all(bf16[32,2,6,2048]{3,1,2,0:T(2,128)(2,1)S(1)} %copy.58), channel_id=1, replica_groups=mesh['pipe'=4,'exp'=16,'pair'=2] {'exp','pair'}, dimensions={0} | all-to-all | bytes 3145728 | tf_op jit(solution)/shard_map/while/body/eval_jaxpr/all_to_all | solution.py:51
  177.0 6.4 fusion.86
  183.4 8.9 %fusion.87 = bf16[32,2,6,2048]{3,0,2,1:T(8,128)(2,1)S(1)} fusion(bf16[2,768,2048]{2,1,0:T(8,128)(2,1)} %get-tuple-element.525, bf16[2,2048,768]{2,1,0:T(8,128)(2,1)} %get-tuple-element.524, bf16[32,2,6,2048]{3,1,2,0:T(2,128)(2,1)S(1)} %all_to_all.26, f32[32,2,6,768]{3,0,2,1:T(8,128)} %fusion.86), kind=kOutput, calls=%fused_computation.10.clone.1 | convolution fusion | flops 2418475008 | bytes 16908288 | tf_op jit(solution)/shard_map/while/body/eval_jaxpr/nlcf,lfd->nlcd/dot_general | solution.py:19
  199.4 22.3 %all-to-all-done.1 = bf16[32,2,6,2048]{3,1,2,0:T(2,128)(2,1)S(1)} async-done(((bf16[32,2,6,2048]{3,1,2,0:T(2,128)(2,1)}), bf16[32,2,6,2048]{3,1,2,0:T(2,128)(2,1)S(1)}, u32[]{:S(2)}, u32[]{:S(2)}) %all-to-all-start.1) | async-done | bytes 1572896 | tf_op jit(solution)/shard_map/while/body/eval_jaxpr/all_to_all | solution.py:56
  223.5 4.3 gather_fusion
  238.0 22.3 %scatter_fusion = bf16[64,6,2048]{2,0,1:T(8,128)(2,1)S(1)} fusion(bf16[64,6,2048]{2,0,1:T(8,128)(2,1)S(1)} %broadcast.267, s32[256]{0:T(256)S(1)} %bitcast.139, bf16[256,2048]{1,0:T(8,128)(2,1)S(1)} %broadcast_bitcast_fusion.2), kind=kCustom, calls=%fused_computation.1.clone.clone.1 | custom fusion | bytes 3147776 | tf_op jit(solution)/shard_map/while/body/eval_jaxpr/scatter | solution.py:48
  263.0 28.1 %all_to_all.26 = bf16[32,2,6,2048]{3,1,2,0:T(2,128)(2,1)S(1)} all-to-all(bf16[32,2,6,2048]{3,1,2,0:T(2,128)(2,1)S(1)} %copy.58), channel_id=1, replica_groups=mesh['pipe'=4,'exp'=16,'pair'=2] {'exp','pair'}, dimensions={0} | all-to-all | bytes 3145728 | tf_op jit(solution)/shard_map/while/body/eval_jaxpr/all_to_all | solution.py:51
  291.2 6.4 fusion.86
  297.6 8.9 %fusion.87 = bf16[32,2,6,2048]{3,0,2,1:T(8,128)(2,1)S(1)} fusion(bf16[2,768,2048]{2,1,0:T(8,128)(2,1)} %get-tuple-element.525, bf16[2,2048,768]{2,1,0:T(8,128)(2,1)} %get-tuple-element.524, bf16[32,2,6,2048]{3,1,2,0:T(2,128)(2,1)S(1)} %all_to_all.26, f32[32,2,6,768]{3,0,2,1:T(8,128)} %fusion.86), kind=kOutput, calls=%fused_computation.10.clone.1 | convolution fusion | flops 2418475008 | bytes 16908288 | tf_op jit(solution)/shard_map/while/body/eval_jaxpr/nlcf,lfd->nlcd/dot_general | solution.py:19
  309.3 4.8 all-to-all-start.1
  314.2 22.2 %all-to-all-done.1 = bf16[32,2,6,2048]{3,1,2,0:T(2,128)(2,1)S(1)} async-done(((bf16[32,2,6,2048]{3,1,2,0:T(2,128)(2,1)}), bf16[32,2,6,2048]{3,1,2,0:T(2,128)(2,1)S(1)}, u32[]{:S(2)}, u32[]{:S(2)}) %all-to-all-start.1) | async-done | bytes 1572896 | tf_op jit(solution)/shard_map/while/body/eval_jaxpr/all_to_all | solution.py:56
  352.7 22.3 %scatter_fusion = bf16[64,6,2048]{2,0,1:T(8,128)(2,1)S(1)} fusion(bf16[64,6,2048]{2,0,1:T(8,128)(2,1)S(1)} %broadcast.267, s32[256]{0:T(256)S(1)} %bitcast.139, bf16[256,2048]{1,0:T(8,128)(2,1)S(1)} %broadcast_bitcast_fusion.2), kind=kCustom, calls=%fused_computation.1.clone.clone.1 | custom fusion | bytes 3147776 | tf_op jit(solution)/shard_map/while/body/eval_jaxpr/scatter | solution.py:48
  377.8 29.0 %all_to_all.26 = bf16[32,2,6,2048]{3,1,2,0:T(2,128)(2,1)S(1)} all-to-all(bf16[32,2,6,2048]{3,1,2,0:T(2,128)(2,1)S(1)} %copy.58), channel_id=1, replica_groups=mesh['pipe'=4,'exp'=16,'pair'=2] {'exp','pair'}, dimensions={0} | all-to-all | bytes 3145728 | tf_op jit(solution)/shard_map/while/body/eval_jaxpr/all_to_all | solution.py:51
  406.7 6.4 fusion.86
  413.2 8.9 %fusion.87 = bf16[32,2,6,2048]{3,0,2,1:T(8,128)(2,1)S(1)} fusion(bf16[2,768,2048]{2,1,0:T(8,128)(2,1)} %get-tuple-element.525, bf16[2,2048,768]{2,1,0:T(8,128)(2,1)} %get-tuple-element.524, bf16[32,2,6,2048]{3,1,2,0:T(2,128)(2,1)S(1)} %all_to_all.26, f32[32,2,6,768]{3,0,2,1:T(8,128)} %fusion.86), kind=kOutput, calls=%fused_computation.10.clone.1 | convolution fusion | flops 2418475008 | bytes 16908288 | tf_op jit(solution)/shard_map/while/body/eval_jaxpr/nlcf,lfd->nlcd/dot_general | solution.py:19
  424.9 4.8 all-to-all-start.1
  429.8 22.2 %all-to-all-done.1 = bf16[32,2,6,2048]{3,1,2,0:T(2,128)(2,1)S(1)} async-done(((bf16[32,2,6,2048]{3,1,2,0:T(2,128)(2,1)}), bf16[32,2,6,2048]{3,1,2,0:T(2,128)(2,1)S(1)}, u32[]{:S(2)}, u32[]{:S(2)}) %all-to-all-start.1) | async-done | bytes 1572896 | tf_op jit(solution)/shard_map/while/body/eval_jaxpr/all_to_all | solution.py:56
  453.8 4.3 gather_fusion
  468.3 22.3 %scatter_fusion = bf16[64,6,2048]{2,0,1:T(8,128)(2,1)S(1)} fusion(bf16[64,6,2048]{2,0,1:T(8,128)(2,1)S(1)} %broadcast.267, s32[256]{0:T(256)S(1)} %bitcast.139, bf16[256,2048]{1,0:T(8,128)(2,1)S(1)} %broadcast_bitcast_fusion.2), kind=kCustom, calls=%fused_computation.1.clone.clone.1 | custom fusion | bytes 3147776 | tf_op jit(solution)/shard_map/while/body/eval_jaxpr/scatter | solution.py:48
  493.4 29.0 %all_to_all.26 = bf16[32,2,6,2048]{3,1,2,0:T(2,128)(2,1)S(1)} all-to-all(bf16[32,2,6,2048]{3,1,2,0:T(2,128)(2,1)S(1)} %copy.58), channel_id=1, replica_groups=mesh['pipe'=4,'exp'=16,'pair'=2] {'exp','pair'}, dimensions={0} | all-to-all | bytes 3145728 | tf_op jit(solution)/shard_map/while/body/eval_jaxpr/all_to_all | solution.py:51
  522.4 6.4 fusion.86
  528.8 8.9 %fusion.87 = bf16[32,2,6,2048]{3,0,2,1:T(8,128)(2,1)S(1)} fusion(bf16[2,768,2048]{2,1,0:T(8,128)(2,1)} %get-tuple-element.525, bf16[2,2048,768]{2,1,0:T(8,128)(2,1)} %get-tuple-element.524, bf16[32,2,6,2048]{3,1,2,0:T(2,128)(2,1)S(1)} %all_to_all.26, f32[32,2,6,768]{3,0,2,1:T(8,128)} %fusion.86), kind=kOutput, calls=%fused_computation.10.clone.1 | convolution fusion | flops 2418475008 | bytes 16908288 | tf_op jit(solution)/shard_map/while/body/eval_jaxpr/nlcf,lfd->nlcd/dot_general | solution.py:19
  540.5 4.7 all-to-all-start.1
  545.4 22.2 %all-to-all-done.1 = bf16[32,2,6,2048]{3,1,2,0:T(2,128)(2,1)S(1)} async-done(((bf16[32,2,6,2048]{3,1,2,0:T(2,128)(2,1)}), bf16[32,2,6,2048]{3,1,2,0:T(2,128)(2,1)S(1)}, u32[]{:S(2)}, u32[]{:S(2)}) %all-to-all-start.1) | async-done | bytes 1572896 | tf_op jit(solution)/shard_map/while/body/eval_jaxpr/all_to_all | solution.py:56
  569.4 4.3 gather_fusion
  583.9 22.3 %scatter_fusion = bf16[64,6,2048]{2,0,1:T(8,128)(2,1)S(1)} fusion(bf16[64,6,2048]{2,0,1:T(8,128)(2,1)S(1)} %broadcast.267, s32[256]{0:T(256)S(1)} %bitcast.139, bf16[256,2048]{1,0:T(8,128)(2,1)S(1)} %broadcast_bitcast_fusion.2), kind=kCustom, calls=%fused_computation.1.clone.clone.1 | custom fusion | bytes 3147776 | tf_op jit(solution)/shard_map/while/body/eval_jaxpr/scatter | solution.py:48
  609.0 29.0 %all_to_all.26 = bf16[32,2,6,2048]{3,1,2,0:T(2,128)(2,1)S(1)} all-to-all(bf16[32,2,6,2048]{3,1,2,0:T(2,128)(2,1)S(1)} %copy.58), channel_id=1, replica_groups=mesh['pipe'=4,'exp'=16,'pair'=2] {'exp','pair'}, dimensions={0} | all-to-all | bytes 3145728 | tf_op jit(solution)/shard_map/while/body/eval_jaxpr/all_to_all | solution.py:51
  637.9 6.4 fusion.86
  644.4 8.9 %fusion.87 = bf16[32,2,6,2048]{3,0,2,1:T(8,128)(2,1)S(1)} fusion(bf16[2,768,2048]{2,1,0:T(8,128)(2,1)} %get-tuple-element.525, bf16[2,2048,768]{2,1,0:T(8,128)(2,1)} %get-tuple-element.524, bf16[32,2,6,2048]{3,1,2,0:T(2,128)(2,1)S(1)} %all_to_all.26, f32[32,2,6,768]{3,0,2,1:T(8,128)} %fusion.86), kind=kOutput, calls=%fused_computation.10.clone.1 | convolution fusion | flops 2418475008 | bytes 16908288 | tf_op jit(solution)/shard_map/while/body/eval_jaxpr/nlcf,lfd->nlcd/dot_general | solution.py:19
  656.0 4.7 all-to-all-start.1
  661.0 22.2 %all-to-all-done.1 = bf16[32,2,6,2048]{3,1,2,0:T(2,128)(2,1)S(1)} async-done(((bf16[32,2,6,2048]{3,1,2,0:T(2,128)(2,1)}), bf16[32,2,6,2048]{3,1,2,0:T(2,128)(2,1)S(1)}, u32[]{:S(2)}, u32[]{:S(2)}) %all-to-all-start.1) | async-done | bytes 1572896 | tf_op jit(solution)/shard_map/while/body/eval_jaxpr/all_to_all | solution.py:56
  685.0 4.3 gather_fusion
  699.5 22.3 %scatter_fusion = bf16[64,6,2048]{2,0,1:T(8,128)(2,1)S(1)} fusion(bf16[64,6,2048]{2,0,1:T(8,128)(2,1)S(1)} %broadcast.267, s32[256]{0:T(256)S(1)} %bitcast.139, bf16[256,2048]{1,0:T(8,128)(2,1)S(1)} %broadcast_bitcast_fusion.2), kind=kCustom, calls=%fused_computation.1.clone.clone.1 | custom fusion | bytes 3147776 | tf_op jit(solution)/shard_map/while/body/eval_jaxpr/scatter | solution.py:48
  724.5 28.9 %all_to_all.26 = bf16[32,2,6,2048]{3,1,2,0:T(2,128)(2,1)S(1)} all-to-all(bf16[32,2,6,2048]{3,1,2,0:T(2,128)(2,1)S(1)} %copy.58), channel_id=1, replica_groups=mesh['pipe'=4,'exp'=16,'pair'=2] {'exp','pair'}, dimensions={0} | all-to-all | bytes 3145728 | tf_op jit(solution)/shard_map/while/body/eval_jaxpr/all_to_all | solution.py:51
  753.4 6.4 fusion.86
  759.9 8.9 %fusion.87 = bf16[32,2,6,2048]{3,0,2,1:T(8,128)(2,1)S(1)} fusion(bf16[2,768,2048]{2,1,0:T(8,128)(2,1)} %get-tuple-element.525, bf16[2,2048,768]{2,1,0:T(8,128)(2,1)} %get-tuple-element.524, bf16[32,2,6,2048]{3,1,2,0:T(2,128)(2,1)S(1)} %all_to_all.26, f32[32,2,6,768]{3,0,2,1:T(8,128)} %fusion.86), kind=kOutput, calls=%fused_computation.10.clone.1 | convolution fusion | flops 2418475008 | bytes 16908288 | tf_op jit(solution)/shard_map/while/body/eval_jaxpr/nlcf,lfd->nlcd/dot_general | solution.py:19
  771.6 4.7 all-to-all-start.1
  776.5 22.2 %all-to-all-done.1 = bf16[32,2,6,2048]{3,1,2,0:T(2,128)(2,1)S(1)} async-done(((bf16[32,2,6,2048]{3,1,2,0:T(2,128)(2,1)}), bf16[32,2,6,2048]{3,1,2,0:T(2,128)(2,1)S(1)}, u32[]{:S(2)}, u32[]{:S(2)}) %all-to-all-start.1) | async-done | bytes 1572896 | tf_op jit(solution)/shard_map/while/body/eval_jaxpr/all_to_all | solution.py:56
  (221 shorter events, 134.4 us)
Async XLA Ops:
  79.9 4.5 copy-start
  79.9 25.4 %all-to-all-start.1 = ((bf16[32,2,6,2048]{3,1,2,0:T(2,128)(2,1)}), bf16[32,2,6,2048]{3,1,2,0:T(2,128)(2,1)S(1)}, u32[]{:S(2)}, u32[]{:S(2)}) async-start(bf16[32,2,6,2048]{3,1,2,0:T(2,128)(2,1)} %copy.59), calls=%async_computation.1 | async-start | bytes 3145728 | tf_op jit(solution)/shard_map/while/body/eval_jaxpr/all_to_all | solution.py:56
  113.5 9.4 %collective-permute-start = (bf16[32,2048]{1,0:T(8,128)(2,1)S(1)}, bf16[32,2048]{1,0:T(8,128)(2,1)S(1)}, u32[]{:S(2)}, u32[]{:S(2)}) collective-permute-start(bf16[32,2048]{1,0:T(8,128)(2,1)S(1)} %get-tuple-element.478), channel_id=1, source_target_pairs={{0,32},{32,64},{64,96},{1,33},{33,65},{65,97},{2,34},{34,66},{66,9... | collective-permute-start | bytes 393224 | tf_op jit(solution)/shard_map/while/body/eval_jaxpr/ppermute | solution.py:12
  195.1 4.1 copy-start
  195.1 26.5 %all-to-all-start.1 = ((bf16[32,2,6,2048]{3,1,2,0:T(2,128)(2,1)}), bf16[32,2,6,2048]{3,1,2,0:T(2,128)(2,1)S(1)}, u32[]{:S(2)}, u32[]{:S(2)}) async-start(bf16[32,2,6,2048]{3,1,2,0:T(2,128)(2,1)} %copy.59), calls=%async_computation.1 | async-start | bytes 3145728 | tf_op jit(solution)/shard_map/while/body/eval_jaxpr/all_to_all | solution.py:56
  229.9 3.9 collective-permute-start
  309.3 4.8 copy-start
  309.3 27.2 %all-to-all-start.1 = ((bf16[32,2,6,2048]{3,1,2,0:T(2,128)(2,1)}), bf16[32,2,6,2048]{3,1,2,0:T(2,128)(2,1)S(1)}, u32[]{:S(2)}, u32[]{:S(2)}) async-start(bf16[32,2,6,2048]{3,1,2,0:T(2,128)(2,1)} %copy.59), calls=%async_computation.1 | async-start | bytes 3145728 | tf_op jit(solution)/shard_map/while/body/eval_jaxpr/all_to_all | solution.py:56
  344.7 3.8 collective-permute-start
  424.9 4.8 copy-start
  424.9 27.2 %all-to-all-start.1 = ((bf16[32,2,6,2048]{3,1,2,0:T(2,128)(2,1)}), bf16[32,2,6,2048]{3,1,2,0:T(2,128)(2,1)S(1)}, u32[]{:S(2)}, u32[]{:S(2)}) async-start(bf16[32,2,6,2048]{3,1,2,0:T(2,128)(2,1)} %copy.59), calls=%async_computation.1 | async-start | bytes 3145728 | tf_op jit(solution)/shard_map/while/body/eval_jaxpr/all_to_all | solution.py:56
  460.2 3.8 collective-permute-start
  540.5 4.8 copy-start
  540.5 27.2 %all-to-all-start.1 = ((bf16[32,2,6,2048]{3,1,2,0:T(2,128)(2,1)}), bf16[32,2,6,2048]{3,1,2,0:T(2,128)(2,1)S(1)}, u32[]{:S(2)}, u32[]{:S(2)}) async-start(bf16[32,2,6,2048]{3,1,2,0:T(2,128)(2,1)} %copy.59), calls=%async_computation.1 | async-start | bytes 3145728 | tf_op jit(solution)/shard_map/while/body/eval_jaxpr/all_to_all | solution.py:56
  575.8 3.8 collective-permute-start
  656.0 4.8 copy-start
  656.0 27.2 %all-to-all-start.1 = ((bf16[32,2,6,2048]{3,1,2,0:T(2,128)(2,1)}), bf16[32,2,6,2048]{3,1,2,0:T(2,128)(2,1)S(1)}, u32[]{:S(2)}, u32[]{:S(2)}) async-start(bf16[32,2,6,2048]{3,1,2,0:T(2,128)(2,1)} %copy.59), calls=%async_computation.1 | async-start | bytes 3145728 | tf_op jit(solution)/shard_map/while/body/eval_jaxpr/all_to_all | solution.py:56
  691.4 3.8 collective-permute-start
  771.6 4.8 copy-start
  771.6 27.2 %all-to-all-start.1 = ((bf16[32,2,6,2048]{3,1,2,0:T(2,128)(2,1)}), bf16[32,2,6,2048]{3,1,2,0:T(2,128)(2,1)S(1)}, u32[]{:S(2)}, u32[]{:S(2)}) async-start(bf16[32,2,6,2048]{3,1,2,0:T(2,128)(2,1)} %copy.59), calls=%async_computation.1 | async-start | bytes 3145728 | tf_op jit(solution)/shard_map/while/body/eval_jaxpr/all_to_all | solution.py:56
  806.9 3.8 collective-permute-start
where the time goes:
time: 813 us; the launch traced here: 811 us
  local copies, waits for them, and re-layouts  250 us (31%)
  blocking collectives  200 us (25%)
  waiting for transfers between devices  168 us (21%)
  matrix products  110 us (14%)
  starting transfers between devices  51.3 us (6%)
  other arithmetic  30.6 us (4%)
    all_to_all x7, blocking collectives, layer(): lax.all_to_all(grouped, ('exp', 'pair'), split_axis=0, concat_axis=0, til...  200 us
    scatter x7, local copies, waits for them, and re-layouts, layer(): outgoing.at[chosen, slots].set(jnp.repeat(normed, top_count, axis=0))  156 us
    all_to_all x7, waiting for transfers between devices, layer(): lax.all_to_all(produced, ('exp', 'pair'), split_axis=0, concat_axis=0, ti...  154 us
    dot_general x7, matrix products, expert_block(): jnp.einsum('nlcf,lfd->nlcd', hidden, wdown, preferred_element_type=jnp.fl...  62.2 us
    dot_general x7, matrix products, expert_block(): jnp.einsum('nlcd,ldf->nlcf', arrived, wgate, preferred_element_type=jnp.f...  45 us
    all_to_all x7, starting transfers between devices, layer(): lax.all_to_all(produced, ('exp', 'pair'), split_axis=0, concat_axis=0, ti...  32.4 us
    gather x7, local copies, waits for them, and re-layouts, layer(): results = returned.reshape(experts, capacity, width)[chosen, slots]  30.1 us
    convert_element_type x7, local copies, waits for them, and re-layouts, expert_block(): jnp.einsum('nlcf,lfd->nlcd', hidden, wdown, preferred_element_type=jnp.fl...  19.5 us
  transfers between devices with their start and end apart: 14, of which 14 were waited for; matrix products, arithmetic and copies ran while one was open for 0% of the time, Pallas kernels for 0%

commit v1 on v0

v1 whole, which is shorter than its diff:
```python
import functools

import jax
import jax.numpy as jnp
from jax import lax
from jax.experimental import pallas as pl
from jax.experimental.pallas import tpu as pltpu
from jax.sharding import PartitionSpec as P

EPS = 1e-06
MESH = pl.DeviceIdType.MESH
SIDE = 4
BLOCKS = 2 * SIDE
CAP = 6
F32 = jnp.float32
BF16 = jnp.bfloat16


def kernel(
    sizes,
    hidden_ref, routes_ref, probs_ref, gain_ref, wg_hbm, wu_hbm, wd_hbm,
    out_ref,
    wg, wu, wd, hs, meta, grid, gmeta, outbox, inbox, back, part, parts, ysend, yrecv, acc,
    xin, hid, meta_t, pick, mix, expect, perm, perm_t,
    w_sem, h_r, h_s, y_r, ym_r, g_r, gm_r, g_s, gm_s, x_r, x_s, r_r, r_s, p_r, p_s, f_r, f_s,
):
    micro, tok, width, ff, local, stages = sizes
    half = width // 2
    rows = BLOCKS * CAP
    chunk = local * rows
    stage = lax.axis_index("pipe")
    e = lax.axis_index("exp")
    y = lax.axis_index("pair")
    x, z = e // SIDE, e % SIDE
    gather_at, send_at = (x, z), (z, x)

    def on_x(d):
        return {"exp": (x + d) % SIDE * SIDE + z}

    def on_z(d):
        return {"exp": x * SIDE + (z + d) % SIDE}

    gather_to, send_to = (on_x, on_z), (on_z, on_x)
    y_peer = {"pair": 1 - y}

    def push(src, dst, send, recv, to):
        pltpu.make_async_remote_copy(
            src_ref=src, dst_ref=dst, send_sem=send, recv_sem=recv, device_id=to, device_id_type=MESH
        ).start()

    def await_bytes(ref, sem):
        pltpu.make_async_copy(ref, ref, sem).wait()

    weight_copies = [
        pltpu.make_async_copy(src.at[0], dst, w_sem.at[i])
        for i, (src, dst) in enumerate(((wg_hbm, wg), (wu_hbm, wu), (wd_hbm, wd)))
    ]
    for copy in weight_copies:
        copy.start()

    barrier = pltpu.get_barrier_semaphore()
    greeted = [y_peer] + [f(d) for f in (on_x, on_z) for d in range(1, SIDE)]
    greeted += [{"pipe": (stage + d) % stages} for d in (1, stages - 1)]
    for to in greeted:
        pl.semaphore_signal(barrier, inc=1, device_id=to, device_id_type=MESH)

    every = micro * tok
    lane = lax.broadcasted_iota(jnp.int32, (every, 128), 1)
    expert = lane % 64
    probs = probs_ref[...]
    named = jnp.zeros((every, 128), F32)
    weight = jnp.zeros((every, 128), F32)
    for k in range(routes_ref.shape[1]):
        hit = routes_ref[:, k : k + 1] == expert
        named = jnp.where(hit, 1.0, named)
        weight = jnp.where(hit, probs[:, k : k + 1], weight)
    weight = weight / jnp.sum(probs, axis=-1, keepdims=True)
    r0 = lax.broadcasted_iota(jnp.int32, (every, every), 0)
    r1 = lax.broadcasted_iota(jnp.int32, (every, every), 1)
    earlier = jnp.where((r1 < r0) & (r1 // tok == r0 // tok), 1.0, 0.0).astype(BF16)
    before = jnp.dot(earlier, named.astype(BF16), preferred_element_type=F32)
    both = jnp.where(lane < 64, named * (before + 1.0), weight).astype(BF16)
    for m in range(micro):
        meta[m] = both[m * tok : (m + 1) * tok]

    q0 = lax.broadcasted_iota(jnp.int32, (rows, BLOCKS * tok), 0)
    q1 = lax.broadcasted_iota(jnp.int32, (rows, BLOCKS * tok), 1)
    expect[...] = jnp.where(q0 // CAP == q1 // tok, q0 % CAP + 1, -1).astype(F32)
    total = SIDE * rows
    piece = rows // SIDE
    s0 = lax.broadcasted_iota(jnp.int32, (total, total), 0)
    s1 = lax.broadcasted_iota(jnp.int32, (total, total), 1)
    perm[...] = jnp.where(
        s1 == s0 % rows // piece * rows + s0 // rows * piece + s0 % piece, 1.0, 0.0
    ).astype(BF16)

    pl.semaphore_wait(barrier, len(greeted))

    def normalize(m):
        @pl.when(stage == 0)
        def _():
            hs[m] = hidden_ref[m]

        @pl.when(stage > 0)
        def _():
            await_bytes(hs.at[m], h_r.at[m])

        floated = hs[m].astype(F32)
        scale = lax.rsqrt(jnp.mean(floated * floated, axis=-1, keepdims=True) + EPS)
        normed = (floated * scale * gain_ref[...]).astype(BF16)
        for h in range(2):
            mine = gather_at[h] * 2 + y
            grid[h, m, mine] = normed[:, h * half : (h + 1) * half]
            gmeta[h, m, mine] = meta[m]
        for h in range(2):
            mine = gather_at[h] * 2 + y
            block, tag = grid.at[h, m, mine], gmeta.at[h, m, mine]
            push(tag, tag, gm_s.at[h, m], ym_r.at[h, m], y_peer)
            push(block, block, g_s.at[h, m], y_r.at[h, m], y_peer)
        for h in range(2):
            mine = gather_at[h] * 2 + y
            block, tag = grid.at[h, m, mine], gmeta.at[h, m, mine]
            for d in (2, 1, 3):
                push(tag, tag, gm_s.at[h, m], gm_r.at[h, m], gather_to[h](d))
                push(block, block, g_s.at[h, m], g_r.at[h, m], gather_to[h](d))

    def forward(m):
        for h in range(2):
            other = gather_at[h] * 2 + 1 - y
            block, tag = grid.at[h, m, other], gmeta.at[h, m, other]
            await_bytes(tag, ym_r.at[h, m])
            await_bytes(block, y_r.at[h, m])
            for d in (2, 1, 3):
                push(tag, tag, gm_s.at[h, m], gm_r.at[h, m], gather_to[h](d))
                push(block, block, g_s.at[h, m], g_r.at[h, m], gather_to[h](d))

    def dispatch(m):
        for h in range(2):
            await_bytes(gmeta.at[h, m, 0 : BLOCKS - 2], gm_r.at[h, m])
            tags = gmeta[h, m].reshape(BLOCKS * tok, 128).astype(F32)
            meta_t[h] = tags.T
            for a in range(SIDE):
                owner = (x * SIDE + a) if h == 0 else (a * SIDE + z)
                for l in range(local):
                    at = (owner * 2 + y) * local + l
                    code = meta_t[h, pl.ds(at, 1), :]
                    to = slice((a * local + l) * rows, (a * local + l + 1) * rows)
                    pick[h, to] = jnp.where(code == expect[...], 1.0, 0.0).astype(BF16)
        for h in range(2):
            await_bytes(grid.at[h, m, 0 : BLOCKS - 2], g_r.at[h, m])
            for n in range(0, half, 512):
                chosen = jnp.dot(
                    pick[h],
                    grid[h, m, :, :, n : n + 512].reshape(BLOCKS * tok, 512),
                    preferred_element_type=F32,
                )
                outbox[h, m, :, :, :, n : n + 512] = chosen.astype(BF16).reshape(SIDE, local, rows, 512)
            own = send_at[h]
            for d in (2, 1, 3):
                push(
                    outbox.at[h, m, (own + d) % SIDE], inbox.at[h, m, own],
                    x_s.at[h, m], x_r.at[h, m], send_to[h](d),
                )
            inbox[h, m, own] = outbox[h, m, own]
        for h in range(2):
            for a in range(SIDE):
                owner = (x * SIDE + a) if h == 0 else (a * SIDE + z)
                for l in range(local):
                    at = (owner * 2 + y) * local + l
                    code = meta_t[h, pl.ds(at, 1), :]
                    share = meta_t[h, pl.ds(64 + at, 1), :]
                    to = slice((a * local + l) * rows, (a * local + l + 1) * rows)
                    mix[h, m % 2, to] = jnp.where(code == expect[...], share, 0.0)

    def experts(m):
        for h in range(2):
            await_bytes(inbox.at[h, m, 0 : SIDE - 1], x_r.at[h, m])
            await_bytes(outbox.at[h, m, 0 : SIDE - 1], x_s.at[h, m])
        for l in range(local):
            xin[l, :, 0:half] = inbox[0, m, :, l].reshape(total, half)
            for n in range(0, half, 512):
                turned = jnp.dot(
                    perm[...], inbox[1, m, :, l, :, n : n + 512].reshape(total, 512), preferred_element_type=F32
                )
                xin[l, :, half + n : half + n + 512] = turned.astype(BF16)
        for l in range(local):
            for n in range(0, ff, 256):
                gate = jnp.dot(xin[l], wg[l, :, n : n + 256], preferred_element_type=F32)
                upward = jnp.dot(xin[l], wu[l, :, n : n + 256], preferred_element_type=F32)
                hid[l, :, n : n + 256] = (jax.nn.silu(gate) * upward).astype(BF16)
        for h in range(2):
            for l in range(local):
                hidden = hid[l]
                if h == 1:
                    hidden = jnp.dot(perm[...], hidden, preferred_element_type=F32).astype(BF16)
                for n in range(0, half, 256):
                    made = jnp.dot(hidden, wd[l, :, h * half + n : h * half + n + 256], preferred_element_type=F32)
                    outbox[h, m, :, l, :, n : n + 256] = made.astype(BF16).reshape(SIDE, rows, 256)
            own = send_at[h]
            for d in (2, 1, 3):
                push(
                    outbox.at[h, m, (own + d) % SIDE], back.at[h, m, own],
                    r_s.at[h, m], r_r.at[h, m], send_to[h](d),
                )
            back[h, m, own] = outbox[h, m, own]

    def combine(m):
        for h in range(2):
            await_bytes(back.at[h, m, 0 : SIDE - 1], r_r.at[h, m])
            shares = mix[h, m % 2].T.astype(BF16)
            for n in range(0, half, 512):
                summed = jnp.dot(
                    shares,
                    back[h, m, :, :, :, n : n + 512].reshape(SIDE * chunk, 512),
                    preferred_element_type=F32,
                )
                part[h, m, :, :, n : n + 512] = summed.astype(BF16).reshape(SIDE, 2 * tok, 512)
            own = gather_at[h]
            for d in (2, 1, 3):
                push(
                    part.at[h, m, (own + d) % SIDE], parts.at[h, m, own],
                    p_s.at[h, m], p_r.at[h, m], gather_to[h](d),
                )

    def reduce(m):
        for h in range(2):
            await_bytes(parts.at[h, m, 0 : SIDE - 1], p_r.at[h, m])
            own = gather_at[h]

            def total_of(side):
                at = pl.ds(pl.multiple_of(side * tok, tok), tok)
                value = part[h, m, own, at].astype(F32)
                for d in range(1, SIDE):
                    value = value + parts[h, m, (own + d) % SIDE, at].astype(F32)
                return value

            ysend[h, m] = total_of(1 - y).astype(BF16)
            push(ysend.at[h, m], yrecv.at[h, m], f_s.at[h, m], f_r.at[h, m], y_peer)
            acc[h] = total_of(y)

    def finish(m):
        for h in range(2):
            await_bytes(yrecv.at[h, m], f_r.at[h, m])
            at = slice(h * half, (h + 1) * half)
            out_ref[m, :, at] = (hs[m, :, at].astype(F32) + (acc[h] + yrecv[h, m].astype(F32))).astype(BF16)

        @pl.when(stage < stages - 1)
        def _():
            push(out_ref.at[m], hs.at[m], h_s.at[m], h_r.at[m], {"pipe": stage + 1})

    def step(i, _):
        @pl.when(i == 1)
        def _():
            for copy in weight_copies:
                copy.wait()

        @pl.when(i > 0)
        def _():
            experts(i - 1)

        @pl.when(i < micro)
        def _():
            normalize(i)
            forward(i)

        @pl.when(i > 0)
        def _():
            combine(i - 1)

        @pl.when(i < micro)
        def _():
            dispatch(i)

        @pl.when(i > 0)
        def _():
            reduce(i - 1)
            finish(i - 1)

        return 0

    lax.fori_loop(0, micro + 1, step, 0)

    def drain(m, _):
        for h in range(2):
            await_bytes(grid.at[h, m, 0 : BLOCKS - 1], g_s.at[h, m])
            await_bytes(gmeta.at[h, m, 0 : BLOCKS - 1], gm_s.at[h, m])
            await_bytes(outbox.at[h, m, 0 : SIDE - 1], r_s.at[h, m])
            await_bytes(part.at[h, m, 0 : SIDE - 1], p_s.at[h, m])
            await_bytes(ysend.at[h, m], f_s.at[h, m])

        @pl.when(stage < stages - 1)
        def _():
            await_bytes(out_ref.at[m], h_s.at[m])

        return 0

    lax.fori_loop(0, micro, drain, 0)


def on_device(stages, hidden_in, routes, gate_probs, norm_gain, w_gate, w_up, w_down):
    micro, tok, width = hidden_in.shape
    top = routes.shape[3]
    local, ff = w_gate.shape[1], w_gate.shape[3]
    half = width // 2
    rows = BLOCKS * CAP
    sizes = (micro, tok, width, ff, local, stages)
    vmem = pl.BlockSpec(memory_space=pltpu.VMEM)
    hbm = pl.BlockSpec(memory_space=pl.ANY)
    pair = pltpu.SemaphoreType.DMA((2, micro))
    single = pltpu.SemaphoreType.DMA((micro,))
    out = pl.pallas_call(
        functools.partial(kernel, sizes),
        out_shape=jax.ShapeDtypeStruct((micro, tok, width), BF16),
        in_specs=[vmem, vmem, vmem, vmem, hbm, hbm, hbm],
        out_specs=vmem,
        scratch_shapes=[
            pltpu.VMEM((local, width, ff), BF16),
            pltpu.VMEM((local, width, ff), BF16),
            pltpu.VMEM((local, ff, width), BF16),
            pltpu.VMEM((micro, tok, width), BF16),
            pltpu.VMEM((micro, tok, 128), BF16),
            pltpu.VMEM((2, micro, BLOCKS, tok, half), BF16),
            pltpu.VMEM((2, micro, BLOCKS, tok, 128), BF16),
            pltpu.VMEM((2, micro, SIDE, local, rows, half), BF16),
            pltpu.VMEM((2, micro, SIDE, local, rows, half), BF16),
            pltpu.VMEM((2, micro, SIDE, local, rows, half), BF16),
            pltpu.VMEM((2, micro, SIDE, 2 * tok, half), BF16),
            pltpu.VMEM((2, micro, SIDE, 2 * tok, half), BF16),
            pltpu.VMEM((2, micro, tok, half), BF16),
            pltpu.VMEM((2, micro, tok, half), BF16),
            pltpu.VMEM((2, tok, half), F32),
            pltpu.VMEM((local, SIDE * rows, width), BF16),
            pltpu.VMEM((local, SIDE * rows, ff), BF16),
            pltpu.VMEM((2, 128, BLOCKS * tok), F32),
            pltpu.VMEM((2, SIDE * local * rows, BLOCKS * tok), BF16),
            pltpu.VMEM((2, 2, SIDE * local * rows, BLOCKS * tok), F32),
            pltpu.VMEM((rows, BLOCKS * tok), F32),
            pltpu.VMEM((SIDE * rows, SIDE * rows), BF16),
            pltpu.VMEM((8, 128), F32),
            pltpu.SemaphoreType.DMA((3,)),
            single, single, pair, pair, pair, pair, pair, pair, pair, pair, pair, pair, pair, pair, pair, pair,
        ],
        compiler_params=pltpu.CompilerParams(
            collective_id=0, has_side_effects=True, vmem_limit_bytes=67043328
        ),
        name="relay",
    )(
        hidden_in,
        routes.reshape(micro * tok, top),
        gate_probs.reshape(micro * tok, top),
        norm_gain,
        w_gate,
        w_up,
        w_down,
    )
    return out[None]


def solution(mesh):
    in_specs = (
        P(None, ("exp", "pair"), None),
        P("pipe", None, ("exp", "pair"), None),
        P("pipe", None, ("exp", "pair"), None),
        P("pipe", None),
        P("pipe", ("exp", "pair"), None, None),
        P("pipe", ("exp", "pair"), None, None),
        P("pipe", ("exp", "pair"), None, None),
    )
    out_specs = P("pipe", None, ("exp", "pair"), None)
    return jax.shard_map(
        functools.partial(on_device, mesh.shape["pipe"]),
        mesh=mesh,
        in_specs=in_specs,
        out_specs=out_specs,
        check_vma=False,
    )
```

time: 813 us -> 270 us (0.33)
  the two profiles are of different devices: /device:TPU:1 before, /device:TPU:17 now
where the time goes in v1:
time: 270 us; the launch traced here: 269 us
  Pallas kernels  264 us (98%)
  local copies, waits for them, and re-layouts  4.73 us (2%)
    pallas_call x1, Pallas kernels, on_device(): pl.pallas_call(functools.partial(kernel, sizes), out_shape=jax.ShapeDtype...  264 us

profile of v1, /device:TPU:17, one launch (start us, length us, event | category | flops | bytes accessed | tf_op | source)
XLA Modules:
  0.0 269.0 jit_solution(3252871146360569312)
XLA Ops:
  0.0 1.4 copy.8
  1.4 1.4 copy.9
  2.8 264.2 %relay.1 = bf16[4,32,2048]{2,1,0:T(8,128)(2,1)} custom-call(bf16[4,32,2048]{2,1,0:T(8,128)(2,1)} %hidden_ref.1, s32[128,8]{1,0:T(8,128)} %bitcast.4, f32[128,8]{1,0:T(8,128)} %bitcast.5, f32[1,2048]{1,0:T(1,128)} %gain_ref.1, bf16[1,2,2048,768]{3,2,1,0:T(8,128)(2,1)} %wg_hbm.1, bf16[1,2,2048,768]{3,2,1,0:T(8,128)(2,1)} %wu_hbm.1, ...), custom_call_target="tpu_custom_call" | custom-call | tf_op jit(solution)/shard_map/relay/pallas_call | solution.py:311
  267.1 1.9 copy.11

commit v2 on v1

v2 whole, which is shorter than its diff:
```python
import functools

import jax
import jax.numpy as jnp
from jax import lax
from jax.experimental import pallas as pl
from jax.experimental.pallas import tpu as pltpu
from jax.sharding import PartitionSpec as P

EPS = 1e-06
MESH = pl.DeviceIdType.MESH
SIDE = 4
BLOCKS = 2 * SIDE
ORDER = (
    ("normalize", 0), ("prepare", 0), ("combine", 1), ("dispatch", 0), ("reduce", 1), ("finish", 1), ("experts", 0),
)
PIECES = 4
CAP = 6
F32 = jnp.float32
BF16 = jnp.bfloat16


def kernel(
    sizes,
    hidden_ref, routes_ref, probs_ref, gain_ref, wg_hbm, wu_hbm, wd_hbm,
    out_ref,
    wg, wu, wd, hs, grid, gmeta, outbox, inbox, back, part, parts, ysend, yrecv, acc,
    xin, sums, hid, turned, meta_t, pick, mix, shares, expect, perm,
    w_sem, ym_r, gm_r, gm_s, i_s, h_r, h_s, o_r, o_s,
    g_r, g_s, x_r, x_s, r_r, r_s, p_r, p_s, f_r, f_s,
):
    micro, tok, width, ff, local, stages = sizes
    half = width // 2
    span = half // PIECES
    order = [(c, h) for c in range(PIECES) for h in range(2)]
    rows = BLOCKS * CAP
    chunk = local * rows
    stage = lax.axis_index("pipe")
    e = lax.axis_index("exp")
    y = lax.axis_index("pair")
    x, z = e // SIDE, e % SIDE
    gather_at, send_at = (x, z), (z, x)

    def on_x(d):
        return {"exp": (x + d) % SIDE * SIDE + z}

    def on_z(d):
        return {"exp": x * SIDE + (z + d) % SIDE}

    gather_to, send_to = (on_x, on_z), (on_z, on_x)
    y_peer = {"pair": 1 - y}

    def push(src, dst, send, recv, to):
        pltpu.make_async_remote_copy(
            src_ref=src, dst_ref=dst, send_sem=send, recv_sem=recv, device_id=to, device_id_type=MESH
        ).start()

    def await_bytes(ref, sem):
        with jax.named_scope("wait"):
            pltpu.make_async_copy(ref, ref, sem).wait()

    weight_copies = [
        pltpu.make_async_copy(src.at[0], dst, w_sem.at[i])
        for i, (src, dst) in enumerate(((wg_hbm, wg), (wu_hbm, wu), (wd_hbm, wd)))
    ]
    for copy in weight_copies:
        copy.start()

    barrier = pltpu.get_barrier_semaphore()
    greeted = [y_peer] + [f(d) for f in (on_x, on_z) for d in range(1, SIDE)]
    greeted += [{"pipe": (stage + d) % stages} for d in (1, stages - 1)]
    greeted += [{"pipe": (stage + d) % stages, "pair": 1 - y} for d in (1, stages - 1)]
    for to in greeted:
        pl.semaphore_signal(barrier, inc=1, device_id=to, device_id_type=MESH)

    lane = lax.broadcasted_iota(jnp.int32, (tok, 128), 1)
    expert = (lane % 64).astype(F32)
    r0 = lax.broadcasted_iota(jnp.int32, (tok, tok), 0)
    r1 = lax.broadcasted_iota(jnp.int32, (tok, tok), 1)
    earlier = jnp.where(r1 < r0, 1.0, 0.0)
    eye = jnp.where(r1 == r0, 1.0, 0.0)
    last = (((1,), (1,)), ((), ()))
    for m in range(micro):
        chosen = lax.dot_general(eye, routes_ref[m].astype(F32), last, preferred_element_type=F32, precision="highest")
        probs = lax.dot_general(eye, probs_ref[m], last, preferred_element_type=F32, precision="highest")
        named = jnp.zeros((tok, 128), F32)
        weight = jnp.zeros((tok, 128), F32)
        for k in range(routes_ref.shape[1]):
            hit = chosen[:, k : k + 1] == expert
            named = jnp.where(hit, 1.0, named)
            weight = jnp.where(hit, probs[:, k : k + 1], weight)
        weight = weight / jnp.sum(probs, axis=-1, keepdims=True)
        before = jnp.dot(earlier, named, preferred_element_type=F32)
        both = jnp.where(lane < 64, named * (before + 1.0), weight).astype(BF16)
        for h in range(2):
            gmeta[h, gather_at[h] * 2 + y, m] = both

    q0 = lax.broadcasted_iota(jnp.int32, (rows, BLOCKS * tok), 0)
    q1 = lax.broadcasted_iota(jnp.int32, (rows, BLOCKS * tok), 1)
    expect[...] = jnp.where(q0 // CAP == q1 // tok, q0 % CAP + 1, -1).astype(F32)
    total = SIDE * rows
    piece = rows // SIDE
    s0 = lax.broadcasted_iota(jnp.int32, (total, total), 0)
    s1 = lax.broadcasted_iota(jnp.int32, (total, total), 1)
    perm[...] = jnp.where(
        s1 == s0 % rows // piece * rows + s0 // rows * piece + s0 % piece, 1.0, 0.0
    ).astype(BF16)

    @pl.when(stage == 0)
    def _():
        for m in range(micro):
            hs[m, y] = hidden_ref[m]

    with jax.named_scope("greet"):
        pl.semaphore_wait(barrier, len(greeted))

    def offer(m):
        push(hidden_ref.at[m], hs.at[m, y], i_s.at[m], o_r.at[m], y_peer)

    @pl.when(stage == 0)
    def _():
        offer(0)

    for h in range(2):
        tag = gmeta.at[h, gather_at[h] * 2 + y]
        push(tag, tag, gm_s.at[h], ym_r.at[h], y_peer)
        for d in (2, 1, 3):
            push(tag, tag, gm_s.at[h], gm_r.at[h], gather_to[h](d))

    def exchange_tags():
        for h in range(2):
            tag = gmeta.at[h, gather_at[h] * 2 + 1 - y]
            await_bytes(tag, ym_r.at[h])
            for d in (2, 1, 3):
                push(tag, tag, gm_s.at[h], gm_r.at[h], gather_to[h](d))

        for h in range(2):
            await_bytes(gmeta.at[h, 0 : BLOCKS - 2], gm_r.at[h])

    @pl.when(stage > 0)
    def _():
        exchange_tags()

    def prepare(m):
        for h in range(2):
            tags = gmeta[h, :, m].reshape(BLOCKS * tok, 128).astype(F32)
            meta_t[h] = tags.T
            for a in range(SIDE):
                owner = (x * SIDE + a) if h == 0 else (a * SIDE + z)
                for l in range(local):
                    at = (owner * 2 + y) * local + l
                    hit = meta_t[h, pl.ds(at, 1), :] == expect[...]
                    share = meta_t[h, pl.ds(64 + at, 1), :]
                    to = slice((a * local + l) * rows, (a * local + l + 1) * rows)
                    pick[h, to] = jnp.where(hit, 1.0, 0.0).astype(BF16)
                    mix[h, to] = jnp.where(hit, share, 0.0)
            shares[m % 2, h] = mix[h].T.astype(BF16)

    def normalize(m):
        @pl.when(stage > 0)
        def _():
            await_bytes(hs.at[m, y], h_r.at[m])

        for turn in range(2):
            pair = y if turn == 0 else 1 - y
            if turn == 1:
                await_bytes(hs.at[m, pair], o_r.at[m])
            floated = hs[m, pair].astype(F32)
            scale = lax.rsqrt(jnp.mean(floated * floated, axis=-1, keepdims=True) + EPS)
            normed = (floated * scale * gain_ref[...]).astype(BF16)
            for c, h in order:
                at = h * half + c * span
                grid[h, c, m, gather_at[h] * 2 + pair] = normed[:, at : at + span]
            for c, h in order:
                block = grid.at[h, c, m, gather_at[h] * 2 + pair]
                for d in (2, 1, 3):
                    push(block, block, g_s.at[h, c, m], g_r.at[h, c, m], gather_to[h](d))

    def dispatch(m):
        for c, h in order:
            await_bytes(grid.at[h, c, m, 0 : BLOCKS - 2], g_r.at[h, c, m])
            chosen = jnp.dot(
                pick[h], grid[h, c, m].reshape(BLOCKS * tok, span), preferred_element_type=F32
            ).astype(BF16)
            outbox[h, c, m] = chosen.reshape(SIDE, local, rows, span)
            own = send_at[h]
            for d in (2, 1, 3):
                push(
                    outbox.at[h, c, m, (own + d) % SIDE], inbox.at[h, c, m, own],
                    x_s.at[h, c, m], x_r.at[h, c, m], send_to[h](d),
                )
            inbox[h, c, m, own] = outbox[h, c, m, own]

    def experts(m):
        for c in range(PIECES):
            for h in range(2):
                await_bytes(inbox.at[h, c, m, 0 : SIDE - 1], x_r.at[h, c, m])
                await_bytes(outbox.at[h, c, m, 0 : SIDE - 1], x_s.at[h, c, m])
            for l in range(local):
                xin[l] = jnp.dot(
                    perm[...], inbox[1, c, m, :, l].reshape(total, span), preferred_element_type=F32
                ).astype(BF16)
            low, high = slice(c * span, (c + 1) * span), slice(half + c * span, half + (c + 1) * span)
            for l in range(local):
                for n in range(0, ff, 256):
                    to = slice(n, n + 256)
                    gate, upward = [
                        jnp.dot(inbox[0, c, m, :, l].reshape(total, span), w[l, low, to], preferred_element_type=F32)
                        + jnp.dot(xin[l], w[l, high, to], preferred_element_type=F32)
                        for w in (wg, wu)
                    ]
                    if c > 0:
                        gate, upward = gate + sums[0, l, :, to], upward + sums[1, l, :, to]
                    if c < PIECES - 1:
                        sums[0, l, :, to], sums[1, l, :, to] = gate, upward
                    else:
                        hid[l, :, to] = (jax.nn.silu(gate) * upward).astype(BF16)
        for c, h in order:
            for l in range(local):
                if h == 1 and c == 0:
                    turned[l] = jnp.dot(perm[...], hid[l], preferred_element_type=F32).astype(BF16)
                for n in range(0, span, 256):
                    at = h * half + c * span + n
                    made = jnp.dot(
                        hid[l] if h == 0 else turned[l], wd[l, :, at : at + 256], preferred_element_type=F32
                    )
                    outbox[h, c, m, :, l, :, n : n + 256] = made.astype(BF16).reshape(SIDE, rows, 256)
            own = send_at[h]
            for d in (2, 1, 3):
                push(
                    outbox.at[h, c, m, (own + d) % SIDE], back.at[h, c, m, own],
                    r_s.at[h, c, m], r_r.at[h, c, m], send_to[h](d),
                )
            back[h, c, m, own] = outbox[h, c, m, own]

    def combine(m):
        for c, h in order:
            await_bytes(back.at[h, c, m, 0 : SIDE - 1], r_r.at[h, c, m])
            summed = jnp.dot(
                shares[m % 2, h], back[h, c, m].reshape(SIDE * chunk, span), preferred_element_type=F32
            )
            part[h, c, m] = summed.astype(BF16).reshape(SIDE, 2 * tok, span)
            own = gather_at[h]
            for d in (2, 1, 3):
                push(
                    part.at[h, c, m, (own + d) % SIDE], parts.at[h, c, m, own],
                    p_s.at[h, c, m], p_r.at[h, c, m], gather_to[h](d),
                )

    def reduce(m):
        for c, h in order:
            await_bytes(parts.at[h, c, m, 0 : SIDE - 1], p_r.at[h, c, m])
            own = gather_at[h]

            def total_of(side):
                at = pl.ds(pl.multiple_of(side * tok, tok), tok)
                value = part[h, c, m, own, at].astype(F32)
                for d in range(1, SIDE):
                    value = value + parts[h, c, m, (own + d) % SIDE, at].astype(F32)
                return value

            ysend[h, c, m] = total_of(1 - y).astype(BF16)
            push(ysend.at[h, c, m], yrecv.at[h, c, m], f_s.at[h, c, m], f_r.at[h, c, m], y_peer)
            acc[h, c] = total_of(y)

    def finish(m):
        for c, h in order:
            await_bytes(yrecv.at[h, c, m], f_r.at[h, c, m])
            at = slice(h * half + c * span, h * half + (c + 1) * span)
            out_ref[m, :, at] = (
                hs[m, y, :, at].astype(F32) + (acc[h, c] + yrecv[h, c, m].astype(F32))
            ).astype(BF16)

            @pl.when(stage < stages - 1)
            def _():
                done, there = out_ref.at[m, :, at], hs.at[m, y, :, at]
                push(done, there, o_s.at[m], o_r.at[m], {"pipe": stage + 1, "pair": 1 - y})
                push(done, there, h_s.at[m], h_r.at[m], {"pipe": stage + 1})

    tasks = {
        "prepare": prepare, "normalize": normalize, "dispatch": dispatch, "experts": experts,
        "combine": combine, "reduce": reduce, "finish": finish,
    }

    def step(i, _):
        for name, lag in ORDER:

            @pl.when((i >= lag) & (i < micro + lag))
            def _():
                with jax.named_scope(name):
                    if name == "experts":

                        @pl.when(i == lag)
                        def _():
                            for copy in weight_copies:
                                copy.wait()

                    if name == "prepare":

                        @pl.when((i == lag) & (stage == 0))
                        def _():
                            exchange_tags()
                            for m in range(1, micro):
                                offer(m)

                    tasks[name](i - lag)

        return 0

    lax.fori_loop(0, micro + max(lag for _, lag in ORDER), step, 0)

    for h in range(2):
        await_bytes(gmeta.at[h, 0 : BLOCKS - 1], gm_s.at[h])

    def drain(m, _):
        for c, h in order:
            await_bytes(grid.at[h, c, m, 0 : BLOCKS - 2], g_s.at[h, c, m])
            await_bytes(outbox.at[h, c, m, 0 : SIDE - 1], r_s.at[h, c, m])
            await_bytes(part.at[h, c, m, 0 : SIDE - 1], p_s.at[h, c, m])
            await_bytes(ysend.at[h, c, m], f_s.at[h, c, m])

        @pl.when(stage == 0)
        def _():
            await_bytes(hidden_ref.at[m], i_s.at[m])

        @pl.when(stage < stages - 1)
        def _():
            await_bytes(out_ref.at[m], h_s.at[m])
            await_bytes(out_ref.at[m], o_s.at[m])

        return 0

    lax.fori_loop(0, micro, drain, 0)


def on_device(stages, hidden_in, routes, gate_probs, norm_gain, w_gate, w_up, w_down):
    micro, tok, width = hidden_in.shape
    local, ff = w_gate.shape[1], w_gate.shape[3]
    span = width // 2 // PIECES
    rows = BLOCKS * CAP
    sizes = (micro, tok, width, ff, local, stages)
    vmem = pl.BlockSpec(memory_space=pltpu.VMEM)
    hbm = pl.BlockSpec(memory_space=pl.ANY)
    pair = pltpu.SemaphoreType.DMA((2, PIECES, micro))
    halves = pltpu.SemaphoreType.DMA((2,))
    single = pltpu.SemaphoreType.DMA((micro,))
    out = pl.pallas_call(
        functools.partial(kernel, sizes),
        out_shape=jax.ShapeDtypeStruct((micro, tok, width), BF16),
        in_specs=[vmem, vmem, vmem, vmem, hbm, hbm, hbm],
        out_specs=vmem,
        scratch_shapes=[
            pltpu.VMEM((local, width, ff), BF16),
            pltpu.VMEM((local, width, ff), BF16),
            pltpu.VMEM((local, ff, width), BF16),
            pltpu.VMEM((micro, 2, tok, width), BF16),
            pltpu.VMEM((2, PIECES, micro, BLOCKS, tok, span), BF16),
            pltpu.VMEM((2, BLOCKS, micro, tok, 128), BF16),
            pltpu.VMEM((2, PIECES, micro, SIDE, local, rows, span), BF16),
            pltpu.VMEM((2, PIECES, micro, SIDE, local, rows, span), BF16),
            pltpu.VMEM((2, PIECES, micro, SIDE, local, rows, span), BF16),
            pltpu.VMEM((2, PIECES, micro, SIDE, 2 * tok, span), BF16),
            pltpu.VMEM((2, PIECES, micro, SIDE, 2 * tok, span), BF16),
            pltpu.VMEM((2, PIECES, micro, tok, span), BF16),
            pltpu.VMEM((2, PIECES, micro, tok, span), BF16),
            pltpu.VMEM((2, PIECES, tok, span), F32),
            pltpu.VMEM((local, SIDE * rows, span), BF16),
            pltpu.VMEM((2, local, SIDE * rows, ff), F32),
            pltpu.VMEM((local, SIDE * rows, ff), BF16),
            pltpu.VMEM((local, SIDE * rows, ff), BF16),
            pltpu.VMEM((2, 128, BLOCKS * tok), F32),
            pltpu.VMEM((2, SIDE * local * rows, BLOCKS * tok), BF16),
            pltpu.VMEM((2, SIDE * local * rows, BLOCKS * tok), F32),
            pltpu.VMEM((2, 2, BLOCKS * tok, SIDE * local * rows), BF16),
            pltpu.VMEM((rows, BLOCKS * tok), F32),
            pltpu.VMEM((SIDE * rows, SIDE * rows), BF16),
            pltpu.SemaphoreType.DMA((3,)),
            halves, halves, halves, single, single, single, single, single,
            pair, pair, pair, pair, pair, pair, pair, pair, pair, pair,
        ],
        compiler_params=pltpu.CompilerParams(
            collective_id=0, has_side_effects=True, vmem_limit_bytes=67043328
        ),
        name="relay",
    )(
        hidden_in,
        jnp.swapaxes(routes[0], 1, 2),
        jnp.swapaxes(gate_probs[0], 1, 2),
        norm_gain,
        w_gate,
        w_up,
        w_down,
    )
    return out[None]


def solution(mesh):
    in_specs = (
        P(None, ("exp", "pair"), None),
        P("pipe", None, ("exp", "pair"), None),
        P("pipe", None, ("exp", "pair"), None),
        P("pipe", None),
        P("pipe", ("exp", "pair"), None, None),
        P("pipe", ("exp", "pair"), None, None),
        P("pipe", ("exp", "pair"), None, None),
    )
    out_specs = P("pipe", None, ("exp", "pair"), None)
    return jax.shard_map(
        functools.partial(on_device, mesh.shape["pipe"]),
        mesh=mesh,
        in_specs=in_specs,
        out_specs=out_specs,
        check_vma=False,
    )
```

time: 270 us -> 236 us (0.87)
  Pallas kernels: 264 us -> 234 us
  local copies, waits for them, and re-layouts: 4.73 us -> 1.88 us
    pallas_call x1, Pallas kernels: 264 us -> 234 us  [on_device(): pl.pallas_call(functools.partial(kernel, sizes), out_shape=jax.ShapeDtype...]
    unnamed x3 -> x1, local copies, waits for them, and re-layouts: 4.73 us -> 1.88 us
where the time goes in v2:
time: 236 us
  Pallas kernels  234 us (99%)
    pallas_call x1, Pallas kernels, on_device(): pl.pallas_call(functools.partial(kernel, sizes), out_shape=jax.ShapeDtype...  234 us

profile of v2, /device:TPU:17, one launch (start us, length us, event | category | flops | bytes accessed | tf_op | source)
XLA Modules:
  0.0 236.1 jit_solution(10455780173204847688)
XLA Ops:
  0.0 234.2 %relay.1 = bf16[4,32,2048]{2,1,0:T(8,128)(2,1)} custom-call(bf16[4,32,2048]{2,1,0:T(8,128)(2,1)} %hidden_ref.1, s32[4,8,32]{2,1,0:T(8,128)} %bitcast.8, f32[4,8,32]{2,1,0:T(8,128)} %bitcast.9, f32[1,2048]{1,0:T(1,128)} %gain_ref.1, bf16[1,2,2048,768]{3,2,1,0:T(8,128)(2,1)} %wg_hbm.1, bf16[1,2,2048,768]{3,2,1,0:T(8,128)(2,1)} %wu_hbm.1, ...), custom_call_target="tpu_custom_call" | custom-call | tf_op jit(solution)/shard_map/relay/pallas_call | solution.py:347
  234.2 1.9 copy.9

commit v3 on v2

--- a/solution.py
+++ b/solution.py
@@ -127,19 +127,13 @@
         for d in (2, 1, 3):
             push(tag, tag, gm_s.at[h], gm_r.at[h], gather_to[h](d))
 
-    def exchange_tags():
+    with jax.named_scope("tags"):
         for h in range(2):
             tag = gmeta.at[h, gather_at[h] * 2 + 1 - y]
             await_bytes(tag, ym_r.at[h])
             for d in (2, 1, 3):
                 push(tag, tag, gm_s.at[h], gm_r.at[h], gather_to[h](d))
 
-        for h in range(2):
-            await_bytes(gmeta.at[h, 0 : BLOCKS - 2], gm_r.at[h])
-
-    @pl.when(stage > 0)
-    def _():
-        exchange_tags()
 
     def prepare(m):
         for h in range(2):
@@ -297,9 +291,13 @@
 
                     if name == "prepare":
 
+                        @pl.when(i == lag)
+                        def _():
+                            for h in range(2):
+                                await_bytes(gmeta.at[h, 0 : BLOCKS - 2], gm_r.at[h])
+
                         @pl.when((i == lag) & (stage == 0))
                         def _():
-                            exchange_tags()
                             for m in range(1, micro):
                                 offer(m)
 

time: 236 us -> 237 us (level)
  no operation moved by 1% of the time
where the time goes in v3:
time: 237 us; the launch traced here: 236 us
  Pallas kernels  234 us (99%)
    pallas_call x1, Pallas kernels, on_device(): pl.pallas_call(functools.partial(kernel, sizes), out_shape=jax.ShapeDtype...  234 us

profile of v3, /device:TPU:17, one launch (start us, length us, event | category | flops | bytes accessed | tf_op | source)
XLA Modules:
  0.0 236.4 jit_solution(14913302084640906822)
XLA Ops:
  0.0 234.5 %relay.1 = bf16[4,32,2048]{2,1,0:T(8,128)(2,1)} custom-call(bf16[4,32,2048]{2,1,0:T(8,128)(2,1)} %hidden_ref.1, s32[4,8,32]{2,1,0:T(8,128)} %bitcast.8, f32[4,8,32]{2,1,0:T(8,128)} %bitcast.9, f32[1,2048]{1,0:T(1,128)} %gain_ref.1, bf16[1,2,2048,768]{3,2,1,0:T(8,128)(2,1)} %wg_hbm.1, bf16[1,2,2048,768]{3,2,1,0:T(8,128)(2,1)} %wu_hbm.1, ...), custom_call_target="tpu_custom_call" | custom-call | tf_op jit(solution)/shard_map/relay/pallas_call | solution.py:345
  234.5 1.9 copy.9
